TPU v7x, 256 devices: a whole 4x4x8 slice. The times are simulated.
256 devices in a mesh: seq: 32 (over y, z), head: 8 (over x, core).
Axes of the slice: x: 4, y: 4, z: 8, core: 2. Of those that a mesh axis runs over, the one named last changes fastest.
Arguments:
- tokens: bfloat16 [12288, 4096], P('seq', 'head'), may hold values from -6 to 6
- norm_gain: float32 [4096], replicated, may hold values from 0.25 to 1.75
- w_in: bfloat16 [4096, 8, 2304], P('seq', 'head'), may hold values from -0.09375 to 0.09375
- w_dt: bfloat16 [4096, 128], P('seq', 'head'), may hold values from -0.09375 to 0.09375
- dt_bias: float32 [128], P('head'), may hold values from -3 to -1
- a_log: float32 [128], P('head'), may hold values from -11 to -1
- d_skip: float32 [128], P('head'), may hold values from 0.5 to 1.5
- conv_w: float32 [4, 8, 1280], P(None, 'head'), may hold values from -0.5 to 0.5
- conv_b: float32 [8, 1280], P('head'), may hold values from -0.5 to 0.5
- gate_gain: float32 [8, 1024], P('head'), may hold values from 0.25 to 1.75
- w_out: bfloat16 [8, 1024, 4096], P('head'), may hold values from -0.09375 to 0.09375
Outputs:
- mixed: bfloat16 [12288, 4096], P('seq', 'head')
All inputs are finite; a program needn't handle non-finite values.
Results may differ from a plain program's by a relative error of at most 0.018.
Values may be sent and summed in bfloat16 or wider, within the bound.
A program may use at most 128 MiB of HBM per device.

v0:
```python
from functools import partial
import jax
import jax.numpy as jnp
from jax import lax
from jax.sharding import Mesh
from jax.sharding import PartitionSpec as P

STRETCH = 128
SEQ = ("seq_0", "seq_1")
EPS = 1e-05
HIGHEST = lax.Precision.HIGHEST


def from_behind(shard, axis, by):
    count = lax.axis_size(axis)
    pairs = [(i, i + by) for i in range(count) if 0 <= i + by < count]
    return lax.ppermute(shard, axis, pairs)


def sent_together(arrays, axis, dim, along):
    both = jnp.concatenate(arrays, axis=along)
    result, at, gathered = (lax.all_gather(both, axis, axis=dim, tiled=True), 0, [])
    for a in arrays:
        gathered.append(lax.slice_in_dim(result, at, at + a.shape[along], axis=along))
        at += a.shape[along]
    return tuple(gathered)


def neutral_like(shard, identity):
    return jax.tree.map(
        lambda part, zero: jnp.zeros_like(part) + jnp.asarray(zero, part.dtype), shard, identity
    )


def entering(shard, axes, combine, identity):
    before = start = neutral_like(shard, identity)
    running = shard
    for axis in reversed(axes):
        count, index = (lax.axis_size(axis), lax.axis_index(axis))
        pieces = jax.tree.map(
            lambda part, kind: lax.all_gather(part.astype(kind), axis),
            running,
            (jnp.bfloat16, jnp.bfloat16),
        )
        inside, running = (start, start)
        for k in range(count):
            passed = k < index
            running = combine(
                running, jax.tree.map(lambda part, own: part[k].astype(own.dtype), pieces, shard)
            )
            inside = jax.tree.map(lambda new, old: jnp.where(passed, new, old), running, inside)
        before = combine(inside, before)
    return before


def normalize(values, gain):
    squares = jnp.mean(values * values, axis=-1, keepdims=True)
    return values * lax.rsqrt(squares + EPS) * gain


def state_block(inputs, step_size, log_decay, in_map, out_map, block_len):
    length = inputs.shape[0]
    stretch_count = length // block_len
    head_count = inputs.shape[1]
    head_size = inputs.shape[2]
    state_size = in_map.shape[1]
    shaped = (
        inputs.reshape(stretch_count, block_len, head_count, head_size),
        step_size.reshape(stretch_count, block_len, head_count),
        log_decay.reshape(stretch_count, block_len, head_count),
        in_map.reshape(stretch_count, block_len, state_size),
        out_map.reshape(stretch_count, block_len, state_size),
    )
    causal = jnp.arange(block_len)[:, None] >= jnp.arange(block_len)[None, :]

    def advance(state_now, pieces):
        stretch_in, stretch_step, stretch_log, stretch_b, stretch_c = pieces
        cumulative = jnp.cumsum(stretch_log, axis=0)
        gap_log = cumulative[:, None, :] - cumulative[None, :, :]
        decays = jnp.where(
            causal[:, :, None], jnp.exp(jnp.where(causal[:, :, None], gap_log, 0.0)), 0.0
        )
        scores = jnp.dot(stretch_c, stretch_b.T, preferred_element_type=jnp.float32)
        wide_c = stretch_c.astype(jnp.float32)
        wide_b = stretch_b.astype(jnp.float32)
        weights = scores[:, :, None] * decays * stretch_step[None, :, :]
        within = jnp.einsum("ijh,jhp->ihp", weights, stretch_in, precision=HIGHEST)
        across = jnp.exp(cumulative)[:, :, None] * jnp.einsum(
            "in,hpn->ihp", wide_c, state_now, precision=HIGHEST
        )
        to_end = jnp.exp(cumulative[-1][None, :] - cumulative) * stretch_step
        fresh_state = jnp.einsum("jh,jhp,jn->hpn", to_end, stretch_in, wide_b, precision=HIGHEST)
        state_next = jnp.exp(cumulative[-1])[:, None, None] * state_now + fresh_state
        return (state_next, within + across)

    start_state = jnp.zeros((head_count, head_size, state_size), jnp.float32)
    final, outputs = lax.scan(advance, start_state, shaped)
    return (outputs.reshape(length, head_count, head_size), final)


def link_states(earlier, later):
    return (earlier[0] + later[0], jnp.exp(later[0])[:, :, None, None] * earlier[1] + later[1])


def body(tokens, norm_gain, w_in, w_dt, dt_bias, a_log, d_skip, conv_w, conv_b, gate_gain, w_out):
    local_rows = tokens.shape[0]
    kernel_len = conv_w.shape[0]
    groups, group_width = gate_gain.shape
    head_count = dt_bias.shape[0]
    per_group = head_count // groups
    head_size = group_width // per_group
    state_size = (conv_b.shape[1] - group_width) // 2
    gathered = lax.all_gather(tokens, "head", axis=1, tiled=True)
    normed = normalize(gathered.astype(jnp.float32), norm_gain).astype(jnp.bfloat16)
    before = from_behind(normed[local_rows - kernel_len + 1 :], SEQ, 1)
    source = jnp.concatenate([before, normed], axis=0)
    span_rows = source.shape[0]
    flat_in = w_in.reshape(w_in.shape[0], groups * w_in.shape[2])
    pieces = sent_together((flat_in, w_dt), SEQ, 0, 1)
    proj_sum = jnp.dot(source, pieces[0], preferred_element_type=jnp.float32)
    step_sum = jnp.dot(source, pieces[1], preferred_element_type=jnp.float32)
    projected = proj_sum.astype(jnp.bfloat16).reshape(span_rows, groups, w_in.shape[2])
    step_size = jax.nn.softplus(step_sum[span_rows - local_rows :] + dt_bias[None, :])
    gate_raw = projected[span_rows - local_rows :, :, :group_width]
    extended = projected[:, :, group_width:]
    summed = conv_b[None, :, :]
    for offset in range(kernel_len):
        summed = summed + conv_w[offset][None, :, :] * extended[
            offset : offset + local_rows
        ].astype(jnp.float32)
    narrow = lax.optimization_barrier(jax.nn.silu(summed).astype(jnp.bfloat16))
    convolved = narrow.astype(jnp.float32)
    inputs = convolved[:, :, :group_width].reshape(local_rows, groups, per_group, head_size)
    in_map = narrow[:, :, group_width : group_width + state_size]
    out_map = narrow[:, :, group_width + state_size :]
    step_grouped = step_size.reshape(local_rows, groups, per_group)
    log_decay = -jnp.exp(a_log).reshape(groups, per_group)[None, :, :] * step_grouped
    run_block = jax.vmap(
        partial(state_block, block_len=STRETCH), in_axes=(1, 1, 1, 1, 1), out_axes=(1, 0)
    )
    local_out, ending = run_block(inputs, step_grouped, log_decay, in_map, out_map)
    totals = jnp.sum(log_decay, axis=0)
    identity = (jnp.zeros_like(totals), jnp.zeros_like(ending))
    prior_decay, incoming = entering((totals, ending), SEQ, link_states, identity)
    cumulative = jnp.exp(jnp.cumsum(log_decay, axis=0))
    carried = (
        jnp.einsum("tgn,ghpn->tghp", out_map.astype(jnp.float32), incoming, precision=HIGHEST)
        * cumulative[:, :, :, None]
    )
    outputs = local_out + carried + d_skip.reshape(groups, per_group)[None, :, :, None] * inputs
    gated = outputs.reshape(local_rows, groups, group_width) * jax.nn.silu(
        gate_raw.astype(jnp.float32)
    )
    normed_out = normalize(gated, gate_gain[None, :, :]).astype(jnp.bfloat16)
    flat_out = normed_out.reshape(local_rows, groups * group_width)
    terms = jnp.dot(
        flat_out,
        w_out.reshape(groups * group_width, w_out.shape[2]),
        preferred_element_type=jnp.float32,
    )
    return lax.psum_scatter(terms.astype(jnp.bfloat16), "head", scatter_dimension=1, tiled=True)


def solution(mesh):
    split = Mesh(mesh.devices.reshape(4, 8, mesh.shape["head"]), ("seq_0", "seq_1", "head"))
    in_specs = (
        P(SEQ, "head"),
        P(),
        P(SEQ, "head", None),
        P(SEQ, "head"),
        P("head"),
        P("head"),
        P("head"),
        P(None, "head", None),
        P("head", None),
        P("head", None),
        P("head", None, None),
    )
    out_specs = P(SEQ, "head")
    return jax.shard_map(body, mesh=split, in_specs=in_specs, out_specs=out_specs, check_vma=False)
```

profile of v0, /device:TPU:8, one launch (start us, length us, event | category | flops | bytes accessed | tf_op | source)
XLA Modules:
  0.0 413.0 jit_solution(1749421173129096668)
XLA Ops:
  10.2 32.1 %all-gather.7.cloned.1.call-done = bf16[384,4096]{1,0:T(8,128)(2,1)} async-done(((bf16[384,512]{1,0:T(8,128)(2,1)}), bf16[384,4096]{1,0:T(8,128)(2,1)}) %all-gather.7.cloned.1.call-update) | async-done | bytes 3145744 | tf_op jit(solution)/shard_map/all_gather | solution.py:113
  42.3 2.7 fusion.45
  46.3 3.5 collective-permute-start
  49.9 4.3 %collective-permute-done = bf16[3,4096]{1,0:T(4,128)(2,1)S(1)} collective-permute-done((bf16[3,4096]{1,0:T(4,128)(2,1)S(1)}, bf16[3,4096]{1,0:T(4,128)(2,1)S(1)}, u32[]{:S(2)}, u32[]{:S(2)}) %collective-permute-start) | collective-permute-done | bytes 24608 | tf_op jit(solution)/shard_map/ppermute | solution.py:17
  54.2 145.0 %all-gather.9.cloned.1.call-done = bf16[4096,2320]{1,0:T(8,128)(2,1)} async-done(((bf16[128,2320]{1,0:T(8,128)(2,1)}), bf16[4096,2320]{1,0:T(8,128)(2,1)}) %all-gather.9.cloned.1.call-update) | async-done | bytes 19005456 | tf_op jit(solution)/shard_map/all_gather | solution.py:22
  199.2 13.4 %fusion.54 = bf16[387,1,2304]{2,0,1:T(8,128)(2,1)S(1)} fusion(bf16[4096,2320]{1,0:T(8,128)(2,1)} %all-gather.9.cloned.1.call-done, bf16[384,4096]{1,0:T(8,128)(2,1)} %copy-done.4, bf16[3,4096]{1,0:T(4,128)(2,1)S(1)} %collective-permute-done), kind=kOutput, calls=%fused_computation.61 | convolution fusion | flops 7311612928 | bytes 23827968 | tf_op jit(solution)/shard_map/dot_general | solution.py:120
  215.5 2.3 fusion.162
  220.2 3.2 copy.55
  223.4 59.6 %while.14 = (s32[]{:T(128)}, f32[1,16,64,128]{3,2,1,0:T(8,128)S(1)}, f32[3,1,128,16,64]{2,0,4,3,1:T(4,128)}, f32[3,1,128,16]{3,2,1,0:T(8,128)S(1)}, f32[3,1,128,...) while((s32[]{:T(128)}, ...), condition=%wide.region_3.4_spmd.clone.clone, body=%wide.region_1.3_spmd.clone.clone.sunk | while | flops 610682880 | bytes 5721559 | solution.py:97
  224.5 3.3 fusion.191
  229.4 13.8 %dynamic_update_slice.7 = f32[3,1,128,16,64]{2,0,4,3,1:T(4,128)} dynamic-update-slice(f32[3,1,128,16,64]{2,0,4,3,1:T(4,128)} %get-tuple-element.246, f32[1,1,128,16,64]{2,0,4,3,1:T(1,128)S(1)} %bitcast.242, s32[]{:T(128)S(6)} %copy.92, s32[]{:T(128)} %constant.25.clone.1..sunk, s32[]{:T(128)} %constant.25.clone.1..sunk, s32[]{:T(128)} %constant.25.clone.1..sunk, s32[]{:T(128)} %constant.25.clone.1..sunk) | dynamic-update-slice | bytes 1048580 | tf_op jit(solution)/shard_map/vmap()/while/body/jit(dynamic_update_index_in_dim)/dynamic_update_slice | solution.py:97
  244.4 3.3 fusion.191
  249.3 13.8 %dynamic_update_slice.7 = f32[3,1,128,16,64]{2,0,4,3,1:T(4,128)} dynamic-update-slice(f32[3,1,128,16,64]{2,0,4,3,1:T(4,128)} %get-tuple-element.246, f32[1,1,128,16,64]{2,0,4,3,1:T(1,128)S(1)} %bitcast.242, s32[]{:T(128)S(6)} %copy.92, s32[]{:T(128)} %constant.25.clone.1..sunk, s32[]{:T(128)} %constant.25.clone.1..sunk, s32[]{:T(128)} %constant.25.clone.1..sunk, s32[]{:T(128)} %constant.25.clone.1..sunk) | dynamic-update-slice | bytes 1048580 | tf_op jit(solution)/shard_map/vmap()/while/body/jit(dynamic_update_index_in_dim)/dynamic_update_slice | solution.py:97
  264.3 3.3 fusion.191
  269.2 13.8 %dynamic_update_slice.7 = f32[3,1,128,16,64]{2,0,4,3,1:T(4,128)} dynamic-update-slice(f32[3,1,128,16,64]{2,0,4,3,1:T(4,128)} %get-tuple-element.246, f32[1,1,128,16,64]{2,0,4,3,1:T(1,128)S(1)} %bitcast.242, s32[]{:T(128)S(6)} %copy.92, s32[]{:T(128)} %constant.25.clone.1..sunk, s32[]{:T(128)} %constant.25.clone.1..sunk, s32[]{:T(128)} %constant.25.clone.1..sunk, s32[]{:T(128)} %constant.25.clone.1..sunk) | dynamic-update-slice | bytes 1048580 | tf_op jit(solution)/shard_map/vmap()/while/body/jit(dynamic_update_index_in_dim)/dynamic_update_slice | solution.py:97
  285.4 15.7 %all-reduce = bf16[128]{0:T(256)(128)(2,1)S(1)} all-reduce(bf16[128]{0:T(256)(128)(2,1)S(1)} %dynamic-update-slice), channel_id=2, replica_groups=mesh['seq_0'=4,'seq_1'=8,'head'=8] {'seq_1'}, use_global_device_ids=true, to_apply=%add | all-reduce | flops 128 | bytes 512
  301.3 21.9 %all-gather.13.cloned.1.call-done = bf16[8,16,64,128]{3,2,1,0:T(8,128)(2,1)} async-done(((bf16[1,16,64,128]{3,2,1,0:T(8,128)(2,1)}), bf16[8,16,64,128]{3,2,1,0:T(8,128)(2,1)}) %all-gather.13.cloned.1.call-update) | async-done | bytes 2097168 | tf_op jit(solution)/shard_map/all_gather | solution.py:41
  323.1 2.8 fusion.106
  326.0 8.1 %all_gather.27 = bf16[4,1,16]{2,1,0:T(2,128)(2,1)S(1)} all-gather(bf16[1,1,16]{2,1,0:T(2,128)(2,1)S(1)} %get-tuple-element.156), channel_id=1, replica_groups=mesh['seq_0'=4,'seq_1'=8,'head'=8] {'seq_0'}, dimensions={0}, use_global_device_ids=true | all-gather | bytes 160 | tf_op jit(solution)/shard_map/all_gather | solution.py:41
  335.8 2.8 transpose.64
  338.7 11.5 %all-gather.11.cloned.1.call-done = bf16[4,1,16,64,128]{4,3,2,1,0:T(8,128)(2,1)} async-done(((bf16[1,1,16,64,128]{4,3,2,1,0:T(8,128)(2,1)}), bf16[4,1,16,64,128]{4,3,2,1,0:T(8,128)(2,1)}) %all-gather.11.cloned.1.call-update) | async-done | bytes 1048592 | tf_op jit(solution)/shard_map/all_gather | solution.py:41
  350.2 4.7 %fusion.69 = f32[384,1,16,64]{0,3,2,1:T(8,128)} fusion(f32[384,1,16,64]{0,3,2,1:T(8,128)S(1)} %transpose.64, f32[384,1,16,64]{0,3,2,1:T(8,128)S(1)} %bitcast.245, f32[16]{0:T(128)S(1)} %copy-done.12, f32[384,16]{0,1:T(8,128)S(1)} %fusion.139, bf16[4,1,16,64,128]{4,3,2,1,0:T(8,128)(2,1)} %all-gather.11.cloned.1.call-done, f32[16]{0:T(128)S(1)} %get-tuple-element.173, ...), kind=kOutput, calls=%fused_computation.78 | convolution fusion | flops 611844096 | bytes 7988108 | tf_op jit(solution)/shard_map/tgn,ghpn->tghp/dot_general | solution.py:147
  357.6 8.7 %fusion.48 = bf16[384,4096]{1,0:T(8,128)(2,1)} fusion(bf16[1,1024,4096]{2,1,0:T(8,128)(2,1)} %param.23, f32[1024]{0:T(1024)S(1)} %bitcast.251, f32[384]{0:T(512)S(1)} %add_rsqrt_fusion, f32[384,1,1024]{2,0,1:T(8,128)S(1)} %copy.63, bf16[387,1,2304]{2,0,1:T(8,128)(2,1)S(1)} %copy-done.2), kind=kOutput, calls=%fused_computation.59 | convolution fusion | flops 3226337280 | bytes 13899776 | tf_op jit(solution)/shard_map/dot_general | solution.py:156
  366.4 40.1 %reduce-scatter.2.cloned.1.call-done = bf16[384,512]{1,0:T(8,128)(2,1)} async-done(((bf16[384,4096]{1,0:T(8,128)(2,1)}), bf16[384,512]{1,0:T(8,128)(2,1)}) %reduce-scatter.2.cloned.1.call-update) | async-done | bytes 393232 | tf_op jit(solution)/shard_map/reduce_scatter | solution.py:161
  (114 shorter events, 24.6 us)
Async XLA Ops:
  6.5 3.6 copy-start.10
  6.5 35.8 %all-gather.7.cloned.1.call-start = ((), (), s32[]{:S(2)}) async-start(), calls=%async_computation.1 | async-start | bytes 3538944 | tf_op jit(solution)/shard_map/all_gather | solution.py:113
  7.3 191.9 %all-gather.9.cloned.1.call-start = ((), (), s32[]{:S(2)}) async-start(), calls=%async_computation.2 | async-start | bytes 20545536 | tf_op jit(solution)/shard_map/all_gather | solution.py:22
  10.1 34.9 %copy-start.7 = (f32[4096]{0:T(1024)S(1)}, f32[4096]{0:T(1024)}, u32[]{:S(2)}) copy-start(f32[4096]{0:T(1024)} %param.14) | copy-start | bytes 49156
  10.1 313.0 %all-gather.13.cloned.1.call-start = ((), (), s32[]{:S(2)}) async-start(), calls=%async_computation.5 | async-start | bytes 2359296 | tf_op jit(solution)/shard_map/all_gather | solution.py:41
  42.3 2.8 copy-start
  45.1 4.6 %copy-start.6 = (f32[4,1,1280]{2,1,0:T(1,128)S(1)}, f32[4,1,1280]{2,1,0:T(1,128)}, u32[]{:S(2)}) copy-start(f32[4,1,1280]{2,1,0:T(1,128)} %param.20) | copy-start | bytes 61444
  45.1 4.7 %copy-start.8 = (f32[1,1280]{1,0:T(1,128)S(1)}, f32[1,1280]{1,0:T(1,128)}, u32[]{:S(2)}) copy-start(f32[1,1280]{1,0:T(1,128)} %param.21) | copy-start | bytes 15364
  46.2 3.5 copy-start.4
  46.3 7.9 %collective-permute-start = (bf16[3,4096]{1,0:T(4,128)(2,1)S(1)}, bf16[3,4096]{1,0:T(4,128)(2,1)S(1)}, u32[]{:S(2)}, u32[]{:S(2)}) collective-permute-start(bf16[3,4096]{1,0:T(4,128)(2,1)S(1)} %slice.201), channel_id=1, source_target_pairs={{0,8},{8,16},{16,24},{24,32},{32,40},{40,48},{48,56},{56,64},{64,7... | collective-permute-start | bytes 73736 | tf_op jit(solution)/shard_map/ppermute | solution.py:17
  212.6 1.3 copy-start.1
  212.6 2.9 copy-start.5
  213.9 3.9 copy-start.3
  213.9 1.5 copy-start.11
  223.4 60.5 %copy-start.13 = (u32[256]{0:T(256)S(1)}, u32[256]{0:T(256)}, u32[]{:S(2)}) copy-start(u32[256]{0:T(256)} %constant.77) | copy-start | bytes 3076
  283.8 66.4 %all-gather.11.cloned.1.call-start = ((), (), s32[]{:S(2)}) async-start(), calls=%async_computation.3 | async-start | bytes 1310720 | tf_op jit(solution)/shard_map/all_gather | solution.py:41
  325.9 80.6 %reduce-scatter.2.cloned.1.call-start = ((), (), s32[]{:S(2)}) async-start(), calls=%async_computation.4 | async-start | bytes 3538944 | tf_op jit(solution)/shard_map/reduce_scatter | solution.py:161
  335.4 14.7 %copy-start.12 = (f32[16]{0:T(128)S(1)}, f32[16]{0:T(128)}, u32[]{:S(2)}) copy-start(f32[16]{0:T(128)} %param.19) | copy-start | bytes 196
  354.9 2.0 copy-start.2
  356.9 0.7 copy-start.9
Sparse Core Ops, SparseCore 0:
  9.2 33.0 all-gather.6
  44.9 154.2 all-gather.8
  283.9 39.1 all-gather.12
  326.1 24.0 all-gather.10
  366.5 39.9 reduce-scatter.1
where the time goes:
time: 415 us; the launch traced here: 413 us
  waiting for transfers between devices  256 us (62%)
  local copies, waits for them, and re-layouts  56.8 us (14%)
  matrix products  45.5 us (11%)
  blocking collectives  23.8 us (6%)
  between operations  14.1 us (3%)
  other arithmetic  13.3 us (3%)
    all_gather x1, waiting for transfers between devices, sent_together(): lax.all_gather(both, axis, axis=dim, tiled=True)  145 us
    dynamic_update_slice x3, local copies, waits for them, and re-layouts, state_block(): final, outputs = lax.scan(advance, start_state, shaped)  41.5 us
    reduce_scatter x1, waiting for transfers between devices, body(): lax.psum_scatter(terms.astype(jnp.bfloat16), 'head', scatter_dimension=1,...  40.1 us
    all_gather x2, waiting for transfers between devices, entering(): lax.all_gather(part.astype(kind), axis)  33.4 us
    all_gather x1, waiting for transfers between devices, body(): gathered = lax.all_gather(tokens, 'head', axis=1, tiled=True)  32.1 us
    unnamed x1, blocking collectives  15.7 us
    dot_general x1, matrix products, body(): proj_sum = jnp.dot(source, pieces[0], preferred_element_type=jnp.float32)  13.4 us
    dot_general x3, matrix products, advance(): within = jnp.einsum('ijh,jhp->ihp', weights, stretch_in, precision=HIGHEST)  9.81 us
  transfers between devices with their start and end apart: 6, of which 6 were waited for; matrix products, arithmetic and copies ran while one was open for 3% of the time, Pallas kernels for 0%

commit v1 on v0

--- a/solution.py
+++ b/solution.py
@@ -110,7 +110,25 @@
     per_group = head_count // groups
     head_size = group_width // per_group
     state_size = (conv_b.shape[1] - group_width) // 2
-    gathered = lax.all_gather(tokens, "head", axis=1, tiled=True)
+    high = jax.lax.axis_size("head")
+    s_next = jax.lax.axis_index("head")
+    out_arr, h_now, mixed_arr = (high, s_next, tokens.shape[1])
+    chunks = tuple(((b, (b + 1) % out_arr) for b in range(out_arr)))
+    gathered = jnp.zeros((*tokens.shape[:1], out_arr * mixed_arr, *tokens.shape[2:]), tokens.dtype)
+    gathered = lax.dynamic_update_slice_in_dim(gathered, tokens, h_now * mixed_arr, axis=1)
+    ledger = tuple(((b, (b - 1) % out_arr) for b in range(out_arr)))
+    piece_now = big = tokens
+    inter = out_arr // 2
+    for c in range(1, inter + 1):
+        piece_now = jax.lax.ppermute(piece_now, "head", chunks)
+        gathered = lax.dynamic_update_slice_in_dim(
+            gathered, piece_now, (h_now - c) % out_arr * mixed_arr, axis=1
+        )
+        if c < out_arr - inter:
+            big = jax.lax.ppermute(big, "head", ledger)
+            gathered = lax.dynamic_update_slice_in_dim(
+                gathered, big, (h_now + c) % out_arr * mixed_arr, axis=1
+            )
     normed = normalize(gathered.astype(jnp.float32), norm_gain).astype(jnp.bfloat16)
     before = from_behind(normed[local_rows - kernel_len + 1 :], SEQ, 1)
     source = jnp.concatenate([before, normed], axis=0)

time: 415 us -> 389 us (0.937)
  waiting for transfers between devices: 256 us -> 213 us
  starting transfers between devices: 3.63 us -> 13 us
  local copies, waits for them, and re-layouts: 56.8 us -> 62.8 us
    all_gather x1, waiting for transfers between devices: 145 us -> 110 us  [sent_together(): lax.all_gather(both, axis, axis=dim, tiled=True)]
    all_gather x1 -> x0, waiting for transfers between devices: 32.1 us -> none  [body(): gathered = lax.all_gather(tokens, 'head', axis=1, tiled=True)]
    ppermute x0 -> x7, waiting for transfers between devices: none -> 23.6 us  [the longest x4 22.7 us: body(): piece_now = jax.lax.ppermute(piece_now, 'head', chunks)]
    ppermute x0 -> x7, starting transfers between devices: none -> 8.88 us  [the longest x3 8.85 us: body(): big = jax.lax.ppermute(big, 'head', ledger)]
    unnamed x35 -> x33, local copies, waits for them, and re-layouts: 6.62 us -> 9.58 us
  transfers between devices with their start and end apart: 6 -> 12, of which waited for: 6 -> 10; matrix products, arithmetic and copies ran while one was open for 3% -> 2% of each run, Pallas kernels for 0% -> 0%
where the time goes in v1:
time: 389 us; the launch traced here: 387 us
  waiting for transfers between devices  213 us (55%)
  local copies, waits for them, and re-layouts  62.8 us (16%)
  matrix products  45.7 us (12%)
  blocking collectives  23.9 us (6%)
  other arithmetic  14.5 us (4%)
  between operations  14.2 us (4%)
  starting transfers between devices  13 us (3%)
    all_gather x1, waiting for transfers between devices, sent_together(): lax.all_gather(both, axis, axis=dim, tiled=True)  110 us
    dynamic_update_slice x3, local copies, waits for them, and re-layouts, state_block(): final, outputs = lax.scan(advance, start_state, shaped)  41.5 us
    reduce_scatter x1, waiting for transfers between devices, body(): lax.psum_scatter(terms.astype(jnp.bfloat16), 'head', scatter_dimension=1,...  40.1 us
    all_gather x2, waiting for transfers between devices, entering(): lax.all_gather(part.astype(kind), axis)  33.4 us
    ppermute x4, waiting for transfers between devices, body(): piece_now = jax.lax.ppermute(piece_now, 'head', chunks)  22.7 us
    unnamed x1, blocking collectives  15.7 us
    dot_general x1, matrix products, body(): proj_sum = jnp.dot(source, pieces[0], preferred_element_type=jnp.float32)  13.4 us
    dot_general x3, matrix products, advance(): within = jnp.einsum('ijh,jhp->ihp', weights, stretch_in, precision=HIGHEST)  9.79 us
  transfers between devices with their start and end apart: 12, of which 10 were waited for; matrix products, arithmetic and copies ran while one was open for 2% of the time, Pallas kernels for 0%

profile of v1, /device:TPU:8, one launch (start us, length us, event | category | flops | bytes accessed | tf_op | source)
XLA Modules:
  0.0 387.4 jit_solution(759592880242687121)
XLA Ops:
  12.4 5.7 %collective-permute-done = bf16[384,512]{1,0:T(8,128)(2,1)S(1)} collective-permute-done((bf16[384,512]{1,0:T(8,128)(2,1)}, bf16[384,512]{1,0:T(8,128)(2,1)S(1)}, u32[]{:S(2)}, u32[]{:S(2)}) %collective-permute-start) | collective-permute-done | bytes 393248 | tf_op jit(solution)/shard_map/ppermute | solution.py:123
  21.0 5.5 %collective-permute-done.2 = bf16[384,512]{1,0:T(8,128)(2,1)S(1)} collective-permute-done((bf16[384,512]{1,0:T(8,128)(2,1)S(1)}, bf16[384,512]{1,0:T(8,128)(2,1)S(1)}, u32[]{:S(2)}, u32[]{:S(2)}) %collective-permute-start.2) | collective-permute-done | bytes 393248 | tf_op jit(solution)/shard_map/ppermute | solution.py:123
  27.6 3.0 collective-permute-start.5
  30.6 4.2 %collective-permute-done.4 = bf16[384,512]{1,0:T(8,128)(2,1)S(1)} collective-permute-done((bf16[384,512]{1,0:T(8,128)(2,1)S(1)}, bf16[384,512]{1,0:T(8,128)(2,1)S(1)}, u32[]{:S(2)}, u32[]{:S(2)}) %collective-permute-start.4) | collective-permute-done | bytes 393248 | tf_op jit(solution)/shard_map/ppermute | solution.py:123
  35.9 7.3 %collective-permute-done.6 = bf16[384,512]{1,0:T(8,128)(2,1)S(1)} collective-permute-done((bf16[384,512]{1,0:T(8,128)(2,1)S(1)}, bf16[384,512]{1,0:T(8,128)(2,1)S(1)}, u32[]{:S(2)}, u32[]{:S(2)}) %collective-permute-start.6) | collective-permute-done | bytes 393248 | tf_op jit(solution)/shard_map/ppermute | solution.py:123
  46.9 4.0 %collective-permute-start.7 = (bf16[3,4096]{1,0:T(4,128)(2,1)S(1)}, bf16[3,4096]{1,0:T(4,128)(2,1)S(1)}, u32[]{:S(2)}, u32[]{:S(2)}) collective-permute-start(bf16[3,4096]{1,0:T(4,128)(2,1)S(1)} %slice.201), channel_id=1, source_target_pairs={{0,8},{8,16},{16,24},{24,32},{32,40},{40,48},{48,56},{56,64},{64,7... | collective-permute-start | bytes 73736 | tf_op jit(solution)/shard_map/ppermute | solution.py:17
  51.0 5.6 %collective-permute-done.7 = bf16[3,4096]{1,0:T(4,128)(2,1)S(1)} collective-permute-done((bf16[3,4096]{1,0:T(4,128)(2,1)S(1)}, bf16[3,4096]{1,0:T(4,128)(2,1)S(1)}, u32[]{:S(2)}, u32[]{:S(2)}) %collective-permute-start.7) | collective-permute-done | bytes 24608 | tf_op jit(solution)/shard_map/ppermute | solution.py:17
  56.7 110.5 %all-gather.6.cloned.1.call-done = bf16[4096,2320]{1,0:T(8,128)(2,1)} async-done(((bf16[128,2320]{1,0:T(8,128)(2,1)}), bf16[4096,2320]{1,0:T(8,128)(2,1)}) %all-gather.6.cloned.1.call-update) | async-done | bytes 19005456 | tf_op jit(solution)/shard_map/all_gather | solution.py:22
  167.1 13.4 %fusion.54 = bf16[387,1,2304]{2,0,1:T(8,128)(2,1)S(1)} fusion(bf16[4096,2320]{1,0:T(8,128)(2,1)} %all-gather.6.cloned.1.call-done, bf16[384,4096]{1,0:T(8,128)(2,1)} %copy-done.3, bf16[3,4096]{1,0:T(4,128)(2,1)S(1)} %collective-permute-done.7), kind=kOutput, calls=%fused_computation.61 | convolution fusion | flops 7311612928 | bytes 23827968 | tf_op jit(solution)/shard_map/dot_general | solution.py:138
  189.4 3.2 copy.55
  192.7 64.6 %while.14 = (s32[]{:T(128)}, f32[1,16,64,128]{3,2,1,0:T(8,128)S(1)}, f32[3,1,128,16,64]{2,0,4,3,1:T(4,128)}, f32[3,1,128,16]{3,2,1,0:T(8,128)}, f32[3,1,128,16]{...) while((s32[]{:T(128)}, ...), condition=%wide.region_3.4_spmd.clone.clone, body=%wide.region_1.3_spmd.clone.clone.sunk | while | flops 610682880 | bytes 5721559 | solution.py:97
  197.1 3.3 fusion.191
  200.4 13.8 %dynamic_update_slice.47 = f32[3,1,128,16,64]{2,0,4,3,1:T(4,128)} dynamic-update-slice(f32[3,1,128,16,64]{2,0,4,3,1:T(4,128)} %get-tuple-element.246, f32[1,1,128,16,64]{2,0,4,3,1:T(1,128)S(1)} %bitcast.242, s32[]{:T(128)S(6)} %copy.100, s32[]{:T(128)} %constant.97.clone.1..sunk, s32[]{:T(128)} %constant.97.clone.1..sunk, s32[]{:T(128)} %constant.97.clone.1..sunk, s32[]{:T(128)} %constant.97.clone.1..sunk) | dynamic-update-slice | bytes 1048580 | tf_op jit(solution)/shard_map/vmap()/while/body/jit(dynamic_update_index_in_dim)/dynamic_update_slice | solution.py:97
  218.6 3.3 fusion.191
  221.9 13.8 %dynamic_update_slice.47 = f32[3,1,128,16,64]{2,0,4,3,1:T(4,128)} dynamic-update-slice(f32[3,1,128,16,64]{2,0,4,3,1:T(4,128)} %get-tuple-element.246, f32[1,1,128,16,64]{2,0,4,3,1:T(1,128)S(1)} %bitcast.242, s32[]{:T(128)S(6)} %copy.100, s32[]{:T(128)} %constant.97.clone.1..sunk, s32[]{:T(128)} %constant.97.clone.1..sunk, s32[]{:T(128)} %constant.97.clone.1..sunk, s32[]{:T(128)} %constant.97.clone.1..sunk) | dynamic-update-slice | bytes 1048580 | tf_op jit(solution)/shard_map/vmap()/while/body/jit(dynamic_update_index_in_dim)/dynamic_update_slice | solution.py:97
  240.2 3.3 fusion.191
  243.4 13.8 %dynamic_update_slice.47 = f32[3,1,128,16,64]{2,0,4,3,1:T(4,128)} dynamic-update-slice(f32[3,1,128,16,64]{2,0,4,3,1:T(4,128)} %get-tuple-element.246, f32[1,1,128,16,64]{2,0,4,3,1:T(1,128)S(1)} %bitcast.242, s32[]{:T(128)S(6)} %copy.100, s32[]{:T(128)} %constant.97.clone.1..sunk, s32[]{:T(128)} %constant.97.clone.1..sunk, s32[]{:T(128)} %constant.97.clone.1..sunk, s32[]{:T(128)} %constant.97.clone.1..sunk) | dynamic-update-slice | bytes 1048580 | tf_op jit(solution)/shard_map/vmap()/while/body/jit(dynamic_update_index_in_dim)/dynamic_update_slice | solution.py:97
  259.6 15.7 %all-reduce = bf16[128]{0:T(256)(128)(2,1)S(1)} all-reduce(bf16[128]{0:T(256)(128)(2,1)S(1)} %dynamic-update-slice), channel_id=2, replica_groups=mesh['seq_0'=4,'seq_1'=8,'head'=8] {'seq_1'}, use_global_device_ids=true, to_apply=%add | all-reduce | flops 128 | bytes 512
  275.5 21.9 %all-gather.10.cloned.1.call-done = bf16[8,16,64,128]{3,2,1,0:T(8,128)(2,1)} async-done(((bf16[1,16,64,128]{3,2,1,0:T(8,128)(2,1)}), bf16[8,16,64,128]{3,2,1,0:T(8,128)(2,1)}) %all-gather.10.cloned.1.call-update) | async-done | bytes 2097168 | tf_op jit(solution)/shard_map/all_gather | solution.py:41
  300.2 8.1 %all_gather.23 = bf16[4,1,16]{2,1,0:T(2,128)(2,1)S(1)} all-gather(bf16[1,1,16]{2,1,0:T(2,128)(2,1)S(1)} %get-tuple-element.156), channel_id=1, replica_groups=mesh['seq_0'=4,'seq_1'=8,'head'=8] {'seq_0'}, dimensions={0}, use_global_device_ids=true | all-gather | bytes 160 | tf_op jit(solution)/shard_map/all_gather | solution.py:41
  312.9 11.6 %all-gather.8.cloned.1.call-done = bf16[4,1,16,64,128]{4,3,2,1,0:T(8,128)(2,1)} async-done(((bf16[1,1,16,64,128]{4,3,2,1,0:T(8,128)(2,1)}), bf16[4,1,16,64,128]{4,3,2,1,0:T(8,128)(2,1)}) %all-gather.8.cloned.1.call-update) | async-done | bytes 1048592 | tf_op jit(solution)/shard_map/all_gather | solution.py:41
  324.5 4.7 %fusion.69 = f32[384,1,16,64]{0,3,2,1:T(8,128)} fusion(f32[384,1,16,64]{0,3,2,1:T(8,128)S(1)} %transpose.71, f32[384,1,16,64]{0,3,2,1:T(8,128)S(1)} %bitcast.245, f32[16]{0:T(128)S(1)} %copy-done.11, f32[384,16]{0,1:T(8,128)S(1)} %fusion.139, bf16[4,1,16,64,128]{4,3,2,1,0:T(8,128)(2,1)} %all-gather.8.cloned.1.call-done, f32[16]{0:T(128)S(1)} %get-tuple-element.173, ...), kind=kOutput, calls=%fused_computation.78 | convolution fusion | flops 611844096 | bytes 7988108 | tf_op jit(solution)/shard_map/tgn,ghpn->tghp/dot_general | solution.py:165
  331.9 8.8 %fusion.48 = bf16[384,4096]{1,0:T(8,128)(2,1)} fusion(bf16[1,1024,4096]{2,1,0:T(8,128)(2,1)} %param.23, f32[1024]{0:T(1024)S(1)} %bitcast.249, f32[384]{0:T(512)S(1)} %add_rsqrt_fusion, f32[384,1,1024]{2,0,1:T(8,128)S(1)} %copy.63, bf16[387,1,2304]{2,0,1:T(8,128)(2,1)S(1)} %copy-done.1), kind=kOutput, calls=%fused_computation.59 | convolution fusion | flops 3226337280 | bytes 13899776 | tf_op jit(solution)/shard_map/dot_general | solution.py:174
  340.7 40.1 %reduce-scatter.2.cloned.1.call-done = bf16[384,512]{1,0:T(8,128)(2,1)} async-done(((bf16[384,4096]{1,0:T(8,128)(2,1)}), bf16[384,512]{1,0:T(8,128)(2,1)}) %reduce-scatter.2.cloned.1.call-update) | async-done | bytes 393232 | tf_op jit(solution)/shard_map/reduce_scatter | solution.py:179
  (132 shorter events, 48.5 us)
Async XLA Ops:
  6.5 160.6 %all-gather.6.cloned.1.call-start = ((), (), s32[]{:S(2)}) async-start(), calls=%async_computation.1 | async-start | bytes 20545536 | tf_op jit(solution)/shard_map/all_gather | solution.py:22
  9.3 18.2 %copy-start.5 = (bf16[384,512]{1,0:T(8,128)(2,1)S(1)}, bf16[384,512]{1,0:T(8,128)(2,1)}, u32[]{:S(2)}) copy-start(bf16[384,512]{1,0:T(8,128)(2,1)} %param.13) | copy-start | bytes 1179652
  9.4 288.0 %all-gather.10.cloned.1.call-start = ((), (), s32[]{:S(2)}) async-start(), calls=%async_computation.4 | async-start | bytes 2359296 | tf_op jit(solution)/shard_map/all_gather | solution.py:41
  9.4 8.6 %collective-permute-start = (bf16[384,512]{1,0:T(8,128)(2,1)}, bf16[384,512]{1,0:T(8,128)(2,1)S(1)}, u32[]{:S(2)}, u32[]{:S(2)}) collective-permute-start(bf16[384,512]{1,0:T(8,128)(2,1)} %param.13), channel_id=1, source_target_pairs={{0,1},{1,2},{2,3},{3,4},{4,5},{5,6},{6,7},{7,0},{8,9},{9,10},{10,1... | collective-permute-start | bytes 1179656 | tf_op jit(solution)/shard_map/ppermute | solution.py:123
  9.4 8.6 %collective-permute-start.1 = (bf16[384,512]{1,0:T(8,128)(2,1)}, bf16[384,512]{1,0:T(8,128)(2,1)S(1)}, u32[]{:S(2)}, u32[]{:S(2)}) collective-permute-start(bf16[384,512]{1,0:T(8,128)(2,1)} %param.13), channel_id=1, source_target_pairs={{0,7},{1,0},{2,1},{3,2},{4,3},{5,4},{6,5},{7,6},{8,15},{9,8},{10,9... | collective-permute-start | bytes 1179656 | tf_op jit(solution)/shard_map/ppermute | solution.py:128
  18.0 8.4 %collective-permute-start.2 = (bf16[384,512]{1,0:T(8,128)(2,1)S(1)}, bf16[384,512]{1,0:T(8,128)(2,1)S(1)}, u32[]{:S(2)}, u32[]{:S(2)}) collective-permute-start(bf16[384,512]{1,0:T(8,128)(2,1)S(1)} %collective-permute-done), channel_id=1, source_target_pairs={{0,1},{1,2},{2,3},{3,4},{4,5},{5,6},{6,7},{7,0},{8,9},{9,10},{10,1... | collective-permute-start | bytes 1179656 | tf_op jit(solution)/shard_map/ppermute | solution.py:123
  18.0 9.6 %collective-permute-start.3 = (bf16[384,512]{1,0:T(8,128)(2,1)S(1)}, bf16[384,512]{1,0:T(8,128)(2,1)S(1)}, u32[]{:S(2)}, u32[]{:S(2)}) collective-permute-start(bf16[384,512]{1,0:T(8,128)(2,1)S(1)} %collective-permute-done.1), channel_id=1, source_target_pairs={{0,7},{1,0},{2,1},{3,2},{4,3},{5,4},{6,5},{7,6},{8,15},{9,8},{10,9... | collective-permute-start | bytes 1179656 | tf_op jit(solution)/shard_map/ppermute | solution.py:128
  26.5 8.4 %collective-permute-start.4 = (bf16[384,512]{1,0:T(8,128)(2,1)S(1)}, bf16[384,512]{1,0:T(8,128)(2,1)S(1)}, u32[]{:S(2)}, u32[]{:S(2)}) collective-permute-start(bf16[384,512]{1,0:T(8,128)(2,1)S(1)} %collective-permute-done.2), channel_id=1, source_target_pairs={{0,1},{1,2},{2,3},{3,4},{4,5},{5,6},{6,7},{7,0},{8,9},{9,10},{10,1... | collective-permute-start | bytes 1179656 | tf_op jit(solution)/shard_map/ppermute | solution.py:123
  27.6 8.3 %collective-permute-start.5 = (bf16[384,512]{1,0:T(8,128)(2,1)S(1)}, bf16[384,512]{1,0:T(8,128)(2,1)S(1)}, u32[]{:S(2)}, u32[]{:S(2)}) collective-permute-start(bf16[384,512]{1,0:T(8,128)(2,1)S(1)} %collective-permute-done.3), channel_id=1, source_target_pairs={{0,7},{1,0},{2,1},{3,2},{4,3},{5,4},{6,5},{7,6},{8,15},{9,8},{10,9... | collective-permute-start | bytes 1179656 | tf_op jit(solution)/shard_map/ppermute | solution.py:128
  34.9 8.4 %collective-permute-start.6 = (bf16[384,512]{1,0:T(8,128)(2,1)S(1)}, bf16[384,512]{1,0:T(8,128)(2,1)S(1)}, u32[]{:S(2)}, u32[]{:S(2)}) collective-permute-start(bf16[384,512]{1,0:T(8,128)(2,1)S(1)} %collective-permute-done.4), channel_id=1, source_target_pairs={{0,1},{1,2},{2,3},{3,4},{4,5},{5,6},{6,7},{7,0},{8,9},{9,10},{10,1... | collective-permute-start | bytes 1179656 | tf_op jit(solution)/shard_map/ppermute | solution.py:123
  35.9 8.1 %copy-start.7 = (f32[4096]{0:T(1024)S(1)}, f32[4096]{0:T(1024)}, u32[]{:S(2)}) copy-start(f32[4096]{0:T(1024)} %param.14) | copy-start | bytes 49156
  44.0 6.9 %copy-start.6 = (f32[4,1,1280]{2,1,0:T(1,128)S(1)}, f32[4,1,1280]{2,1,0:T(1,128)}, u32[]{:S(2)}) copy-start(f32[4,1,1280]{2,1,0:T(1,128)} %param.20) | copy-start | bytes 61444
  44.1 6.9 %copy-start.8 = (f32[1,1280]{1,0:T(1,128)S(1)}, f32[1,1280]{1,0:T(1,128)}, u32[]{:S(2)}) copy-start(f32[1,1280]{1,0:T(1,128)} %param.21) | copy-start | bytes 15364
  45.2 1.7 copy-start.3
  46.9 9.8 %collective-permute-start.7 = (bf16[3,4096]{1,0:T(4,128)(2,1)S(1)}, bf16[3,4096]{1,0:T(4,128)(2,1)S(1)}, u32[]{:S(2)}, u32[]{:S(2)}) collective-permute-start(bf16[3,4096]{1,0:T(4,128)(2,1)S(1)} %slice.201), channel_id=1, source_target_pairs={{0,8},{8,16},{16,24},{24,32},{32,40},{40,48},{48,56},{56,64},{64,7... | collective-permute-start | bytes 73736 | tf_op jit(solution)/shard_map/ppermute | solution.py:17
  180.5 2.9 copy-start.4
  181.9 3.9 copy-start.2
  181.9 1.5 copy-start.10
  192.7 65.4 %copy-start.12 = (u32[256]{0:T(256)S(1)}, u32[256]{0:T(256)}, u32[]{:S(2)}) copy-start(u32[256]{0:T(256)} %constant.128) | copy-start | bytes 3076
  258.0 66.4 %all-gather.8.cloned.1.call-start = ((), (), s32[]{:S(2)}) async-start(), calls=%async_computation.2 | async-start | bytes 1310720 | tf_op jit(solution)/shard_map/all_gather | solution.py:41
  300.2 80.7 %reduce-scatter.2.cloned.1.call-start = ((), (), s32[]{:S(2)}) async-start(), calls=%async_computation.3 | async-start | bytes 3538944 | tf_op jit(solution)/shard_map/reduce_scatter | solution.py:179
  308.8 15.7 %copy-start.11 = (f32[16]{0:T(128)S(1)}, f32[16]{0:T(128)}, u32[]{:S(2)}) copy-start(f32[16]{0:T(128)} %param.19) | copy-start | bytes 196
  329.2 2.0 copy-start.1
  329.2 2.7 copy-start.9
  (1 other events, 1.3 us)
Sparse Core Ops, SparseCore 0:
  9.9 157.1 all-gather.5
  258.2 39.1 all-gather.9
  300.3 24.1 all-gather.7
  340.8 39.9 reduce-scatter.1
